TPU v7x, 32 devices: a whole 2x2x4 slice. The times are simulated.
32 devices in a mesh: group: 2 (over y), ha: 4 (over x, core), wa: 4 (over z).
Axes of the slice: x: 2, y: 2, z: 4, core: 2. Of those that a mesh axis runs over, the one named last changes fastest.
Arguments:
- queries: bfloat16 [4, 32, 32, 1536], P('group', 'ha', 'wa'), parts along dimension 0, may hold values from -6 to 6
- keys: bfloat16 [4, 32, 32, 1536], P('group', 'ha', 'wa'), parts along dimension 0, may hold values from -6 to 6
- values: bfloat16 [4, 32, 32, 1536], P('group', 'ha', 'wa'), parts along dimension 0, may hold values from -6 to 6
- out_grad: bfloat16 [4, 32, 32, 1536], P('group', 'ha', 'wa'), parts along dimension 0, may hold values from -96 to 96
- log_norm: float32 [12, 4, 32, 32], P(None, 'group', 'ha', 'wa'), parts along dimension 1, may hold values from 6.5 to 7.5
- delta_rows: float32 [12, 4, 32, 32], P(None, 'group', 'ha', 'wa'), parts along dimension 1, may hold values from -360 to 360
- text_keys: bfloat16 [64, 1536], P('group'), parts along dimension 0, may hold values from -6 to 6
- text_values: bfloat16 [64, 1536], P('group'), parts along dimension 0, may hold values from -6 to 6
- window_table: int32 [4, 4, 9], replicated, may hold values 0 or 1
Outputs:
- query_grad: bfloat16 [4, 32, 32, 1536], P('group', 'ha', 'wa'), parts along dimension 0
- key_grad: bfloat16 [4, 32, 32, 1536], P('group', 'ha', 'wa'), parts along dimension 0
- value_grad: bfloat16 [4, 32, 32, 1536], P('group', 'ha', 'wa'), parts along dimension 0
- text_key_grad: bfloat16 [64, 1536], P('group'), parts along dimension 0
- text_value_grad: bfloat16 [64, 1536], P('group'), parts along dimension 0
There are 2 independent parts, one for each index of `group`. A program takes and returns all parts, laid end to end along the dimension named above; an argument that names none is the same for every part. Nothing has to cross between parts.
All inputs are finite; a program needn't handle non-finite values.
Results may differ from a plain program's by a relative error of at most 0.001.
The roundings to bfloat16 on the way count: a program that leaves them out, or rounds other values in their place, can miss the bound.
Values may be sent and summed in bfloat16 or wider, within the bound.
A program may use at most 64 MiB of HBM per device.

v0:
```python
import functools
import math

import jax
import jax.numpy as jnp
from jax import lax
from jax.experimental import pallas as pl
from jax.experimental.pallas import tpu as pltpu
from jax.sharding import PartitionSpec as P

HDIM = 128
HALO = 2
GROUPS = 4
MESH = pl.DeviceIdType.MESH
F32 = jnp.float32
BF16 = jnp.bfloat16


def text_plan(n_ha, n_wa, blocks, width):
    plan = []
    for axis, count in (("ha", n_ha), ("wa", n_wa)):
        far = 1
        while far < count:
            if blocks > 1:
                blocks //= 2
                plan.append((axis, far, blocks, width, "rows"))
            elif width % 256 == 0:
                width //= 2
                plan.append((axis, far, blocks, width, "cols"))
            else:
                plan.append((axis, far, blocks, width, "none"))
            far *= 2
    return plan


def to_rows(block, rows):
    return block.astype(F32).reshape(rows, block.shape[-1])


def contract(a, b, dims):
    return lax.dot_general(a, b, (dims, ((), ())), preferred_element_type=F32)


def kernel(
    n_ha, n_wa, plan,
    table, q_ref, k_ref, v_ref, g_ref, norm_ref, delta_ref, tk_ref, tv_ref,
    dq_ref, dk_ref, dv_ref, dtk_ref, dtv_ref,
    stage, hcol, hrow, hcor, ret, rrow, rcor, rcol, own, dq_acc, mask, norm, delta, tx, tb, *rest,
):
    trecv = rest[: len(plan)]
    (col_s, col_r, row_s, row_r, cor_s, cor_r, rr_s, rr_r, rc_s, rc_r, mid_s, mid_r, rq_s, rq_r, t_s, t_r, u_s, u_r) = rest[len(plan):]
    frames, tile, _, width = q_ref.shape
    cells = frames * tile * tile
    text = tk_ref.shape[0]
    heads = width // HDIM
    part = width // GROUPS
    per = heads // GROUPS
    bands = tile // HALO
    rim = ret.shape[2] - 2 * bands
    scale = 1.0 / math.sqrt(HDIM)
    ha, wa = lax.axis_index("ha"), lax.axis_index("wa")
    ha_of = [{"ha": lax.rem(ha + n_ha - 1, n_ha)}, {"ha": lax.rem(ha + 1, n_ha)}]
    wa_of = [{"wa": lax.rem(wa + n_wa - 1, n_wa)}, {"wa": lax.rem(wa + 1, n_wa)}]
    partners, bits = [], []
    for axis, far, _, _, _ in plan:
        at = ha if axis == "ha" else wa
        bit = lax.rem(lax.div(at, far), 2)
        bits.append(bit)
        partners.append({axis: at + far * (1 - 2 * bit)})

    barrier = pltpu.get_barrier_semaphore()
    greeted = ha_of + wa_of + partners
    for other in greeted:
        pl.semaphore_signal(barrier, inc=1, device_id=other, device_id_type=MESH)

    def cols(g):
        return slice(g * part, (g + 1) * part)

    def remote(src, dst, s, r, device):
        return pltpu.make_async_remote_copy(
            src_ref=src, dst_ref=dst, send_sem=s, recv_sem=r, device_id=device, device_id_type=MESH
        )

    border = 2 * bands * frames * HALO * HALO

    def cell_of(j):
        side = lax.div(j, border // 2)
        band = lax.rem(lax.div(j, frames * HALO * HALO), bands)
        frame = lax.rem(lax.div(j, HALO * HALO), frames)
        row = band * HALO + lax.rem(lax.div(j, HALO), HALO)
        col = lax.rem(j, HALO) + side * (tile - HALO)
        return frame * tile * tile + row * tile + col

    lane = lax.broadcasted_iota(jnp.int32, (border, cells), 1)
    pick = (lane == cell_of(lax.broadcasted_iota(jnp.int32, (border, cells), 0))).astype(F32).astype(BF16)
    back_row = lax.broadcasted_iota(jnp.int32, (cells, 3 * border), 0)
    back_lane = lax.broadcasted_iota(jnp.int32, (cells, 3 * border), 1)
    put_back = (back_row == cell_of(lax.rem(back_lane, border))).astype(F32).astype(BF16)

    col_copy, row_copy, cor_copy, rr_copy, rc_copy, mid_copy, rq_copy = {}, {}, {}, {}, {}, {}, {}
    for g in range(GROUPS):
        for kv, ref in enumerate((k_ref, v_ref)):
            full = to_rows(ref[:, :, :, cols(g)], cells).astype(BF16)
            strip = contract(pick, full, ((1,), (0,)))
            stage[g, kv] = strip.reshape(2, bands, frames * HALO * HALO, part).astype(BF16)
        if g == 0:
            pl.semaphore_wait(barrier, len(greeted))
        for d in range(2):
            c = remote(stage.at[g, :, d], hcol.at[g, :, 1 - d], col_s.at[g, d], col_r.at[g, 1 - d], wa_of[d])
            c.start()
            col_copy[g, d] = c
        for v in range(2):
            for kv, ref in enumerate((k_ref, v_ref)):
                lo = v * (tile - HALO)
                c = remote(
                    ref.at[:, lo:lo + HALO, :, cols(g)], hrow.at[g, kv, 1 - v],
                    row_s.at[g, v, kv], row_r.at[g, 1 - v, kv], ha_of[v],
                )
                c.start()
                row_copy[g, v, kv] = c

    square = (cells, cells)
    same = (lax.broadcasted_iota(jnp.int32, square, 0) == lax.broadcasted_iota(jnp.int32, square, 1)).astype(F32)
    for src, dst in ((norm_ref, norm), (delta_ref, delta)):
        dst[...] = lax.dot_general(
            src[...], same, (((0,), (0,)), ((), ())), precision=lax.Precision.HIGHEST, preferred_element_type=F32
        )

    def live(block):
        return table[ha, wa, block].astype(F32)

    at = 0
    for block, rows in ((1, 32), (7, 32), (0, 8), (2, 8), (6, 8), (8, 8), (3, 32), (5, 32)):
        mask[at:at + rows, :] = jnp.full((rows, cells), live(block), F32)
        at += rows
    own_live = live(4)

    def attend(keys, values, h, masking):
        here = slice(h * HDIM, (h + 1) * HDIM)
        qh = to_rows(q_ref[:, :, :, here], cells).astype(BF16)
        gh = to_rows(g_ref[:, :, :, here], cells).astype(BF16)
        s = contract(keys, qh, ((1,), (1,))) * scale
        p = masking(jnp.exp(s - norm[h:h + 1, :]))
        dp = contract(values, gh, ((1,), (1,)))
        ds = (p * (dp - delta[h:h + 1, :])).astype(BF16)
        dv = contract(p.astype(BF16), gh, ((1,), (0,)))
        dk = contract(ds, qh, ((1,), (0,)))
        dq = contract(ds, keys, ((0,), (0,)))
        return dq, dk, dv

    def texts():
        for h in range(heads):
            here = slice(h * HDIM, (h + 1) * HDIM)
            dq, dk, dv = attend(tk_ref[:, here], tv_ref[:, here], h, lambda p: p)
            dq_acc[:, here] = dq
            tx[: text // 8, :, here] = (dk * scale).reshape(text // 8, 8, HDIM)
            tx[text // 8:, :, here] = dv.reshape(text // 8, 8, HDIM)

    def local(g):
        for h in range(g * per, (g + 1) * per):
            here = slice(h * HDIM, (h + 1) * HDIM)
            keys, values = (to_rows(ref[:, :, :, here], cells).astype(BF16) for ref in (k_ref, v_ref))
            dq, dk, dv = attend(keys, values, h, lambda p: p * own_live)
            dq_acc[:, here] += dq
            own[0, :, here] = dk
            own[1, :, here] = dv

    def forward(g):
        for d in range(2):
            col_copy[g, d].wait()
        for d in range(2):
            for v in range(2):
                c = remote(
                    hcol.at[g, :, d, v * (bands - 1)], hcor.at[g, :, 1 - v, d],
                    cor_s.at[g, d, v], cor_r.at[g, d, 1 - v], ha_of[v],
                )
                c.start()
                cor_copy[g, d, v] = c

    def columns(g):
        for h in range(per):
            here = slice(h * HDIM, (h + 1) * HDIM)
            absolute = slice((g * per + h) * HDIM, (g * per + h + 1) * HDIM)
            keys, values = (to_rows(hcol[g, kv, :, :, :, here], border).astype(BF16) for kv in range(2))
            dq, dk, dv = attend(keys, values, g * per + h, lambda p: p * mask[8 * rim:])
            dq_acc[:, absolute] += dq
            ret[g, 0, rim:, :, here] = dk.reshape(2 * bands, 8, HDIM)
            ret[g, 1, rim:, :, here] = dv.reshape(2 * bands, 8, HDIM)
        for d in range(2):
            lo = rim + d * bands
            c = remote(
                ret.at[g, :, lo + 1:lo + bands - 1], rcol.at[g, :, 1 - d, 1:bands - 1],
                mid_s.at[g, d], mid_r.at[g, 1 - d], wa_of[d],
            )
            c.start()
            mid_copy[g, d] = c

    def pieces_pass(g, refs_of, lo, size, weights):
        for h in range(per):
            here = slice(h * HDIM, (h + 1) * HDIM)
            absolute = slice((g * per + h) * HDIM, (g * per + h + 1) * HDIM)
            keys, values = (refs_of(kv, here).astype(BF16) for kv in range(2))
            dq, dk, dv = attend(keys, values, g * per + h, lambda p: p * weights)
            dq_acc[:, absolute] += dq
            ret[g, 0, lo:lo + size, :, here] = dk.reshape(size, 8, HDIM)
            ret[g, 1, lo:lo + size, :, here] = dv.reshape(size, 8, HDIM)

    def strips(g):
        for v in range(2):
            for kv in range(2):
                row_copy[g, v, kv].wait()
        wide = 2 * frames * HALO * tile
        pieces_pass(g, lambda kv, here: to_rows(hrow[g, kv, :, :, :, :, here], wide), 0, wide // 8, mask[:wide])
        half = wide // 16
        for v in range(2):
            c = remote(
                ret.at[g, :, half * v:half * (v + 1)], rrow.at[g, 1 - v], rr_s.at[g, v], rr_r.at[g, 1 - v], ha_of[v]
            )
            c.start()
            rr_copy[g, v] = c

    def corners(g):
        for v in range(2):
            for d in range(2):
                cor_copy[g, d, v].wait()
        pieces_pass(
            g, lambda kv, here: to_rows(hcor[g, kv, :, :, :, here], 32), rim - 4, 4, mask[8 * (rim - 4):8 * rim]
        )
        for v in range(2):
            c = remote(
                ret.at[g, :, rim - 4 + 2 * v:rim - 2 + 2 * v], rcor.at[g, 1 - v],
                rq_s.at[g, v], rq_r.at[g, 1 - v], ha_of[v],
            )
            c.start()
            rq_copy[g, v] = c

    def fold_corners(g):
        for v in range(2):
            rq_copy[g, v].wait()
        for v in range(2):
            for d in range(2):
                at = rim + bands * d + (bands - 1) * v
                for kv in range(2):
                    ret[g, kv, at] += rcor[g, v, kv, d]
                c = remote(
                    ret.at[g, :, at], rcol.at[g, :, 1 - d, v * (bands - 1)],
                    rc_s.at[g, d, v], rc_r.at[g, 1 - d, v], wa_of[d],
                )
                c.start()
                rc_copy[g, d, v] = c

    def fold_rows(g):
        for v in range(2):
            rr_copy[g, v].wait()
        for v in range(2):
            for kv in range(2):
                for f in range(frames):
                    lo = f * tile * tile + v * (tile - HALO) * tile
                    own[kv, lo:lo + HALO * tile, cols(g)] += rrow[g, v, kv, 2 * f:2 * f + 2].reshape(HALO * tile, part)
        dq_ref[:, :, :, cols(g)] = (dq_acc[:, cols(g)] * scale).reshape(frames, tile, tile, part).astype(BF16)

    def fold_cols(g):
        for d in range(2):
            mid_copy[g, d].wait()
            for v in range(2):
                rc_copy[g, d, v].wait()
        for kv, out in enumerate((dk_ref, dv_ref)):
            came = rcol[g, kv].reshape(border, part)
            first = came.astype(BF16)
            left = came - first.astype(F32)
            second = left.astype(BF16)
            third = (left - second.astype(F32)).astype(BF16)
            total = own[kv, :, cols(g)] + contract(
                put_back, jnp.concatenate([first, second, third], 0), ((1,), (0,))
            )
            if kv == 0:
                total = total * scale
            out[:, :, :, cols(g)] = total.reshape(frames, tile, tile, part).astype(BF16)

    region = {"row": 0, "rows": 2 * text // 8, "col": 0, "cols": width}
    sums, regions = [], []

    def text_send(i):
        _, _, rows, wide, how = plan[i]
        regions.append(dict(region))
        row, col, bit = region["row"], region["col"], bits[i]
        send_row, send_col = row, col
        if how == "rows":
            send_row = row + (1 - bit) * rows
            region.update(row=row + bit * rows, rows=rows)
        elif how == "cols":
            send_col = col + (1 - bit) * wide
            region.update(col=col + bit * wide, cols=wide)
        c = remote(area(tx, send_row, rows, send_col, wide), trecv[i], t_s.at[i], t_r.at[i], partners[i])
        c.start()
        sums.append(c)

    def area(ref, row, rows, col, wide):
        lanes = pl.ds(pl.multiple_of(col, 128), wide) if not isinstance(col, int) else pl.ds(col, wide)
        return ref.at[pl.ds(row, rows), :, lanes]

    def mine(ref):
        return area(ref, region["row"], region["rows"], region["col"], region["cols"])

    def text_add(i):
        sums[i].wait()
        kept = mine(tx)
        kept[...] += trecv[i][...]

    gathers = []

    def text_spread(i):
        if i == len(plan) - 1:
            mine(tb)[...] = mine(tx)[...].astype(BF16)
        if plan[i][4] == "none":
            gathers.append(None)
            return
        c = remote(mine(tb), mine(tb), u_s.at[i], u_r.at[i], partners[i])
        c.start()
        gathers.append(c)

    def text_join(i):
        c = gathers.pop()
        if c is not None:
            c.wait()
        region.update(regions[i])

    steps = []
    for i in range(len(plan)):
        steps += [functools.partial(text_send, i), functools.partial(text_add, i)]
    for i in reversed(range(len(plan))):
        steps += [functools.partial(text_spread, i), functools.partial(text_join, i)]
    waiting = []
    for n in range(0, len(steps)):
        if n % 2 == 0:
            waiting.append([steps[n]])
            if n > 0:
                waiting[-1].insert(0, steps[n - 1])
    waiting.append([steps[-1]])

    def text_step():
        if waiting:
            for step in waiting.pop(0):
                step()

    texts()
    text_step()
    local(0)
    local(1)
    text_step()
    local(2)
    local(3)
    strips(0)
    strips(1)
    text_step()
    forward(0)
    columns(0)
    forward(1)
    columns(1)
    corners(0)
    text_step()
    forward(2)
    columns(2)
    corners(1)
    forward(3)
    columns(3)
    corners(2)
    text_step()
    fold_corners(0)
    corners(3)
    strips(2)
    fold_corners(1)
    strips(3)
    fold_corners(2)
    text_step()
    fold_corners(3)
    text_step()
    fold_rows(0)
    fold_rows(1)
    fold_rows(2)
    fold_rows(3)
    fold_cols(0)
    text_step()
    fold_cols(1)
    fold_cols(2)
    fold_cols(3)
    while waiting:
        text_step()
    dtk_ref[...] = to_rows(tb[: text // 8], text).astype(BF16)
    dtv_ref[...] = to_rows(tb[text // 8:], text).astype(BF16)


def hand_on(*refs):
    count = len(refs) // 2
    for source, target in zip(refs[:count], refs[count:]):
        target[...] = source[...]


def solution(mesh):
    n_ha, n_wa = mesh.shape["ha"], mesh.shape["wa"]

    def local(queries, keys, values, out_grad, log_norm, delta_rows, text_keys, text_values, window_table):
        frames, tile, _, width = queries.shape
        heads = width // HDIM
        text = text_keys.shape[0]
        cells = frames * tile * tile
        part = width // GROUPS
        bands = tile // HALO
        block = frames * HALO * HALO
        halo_blocks = (4 * HALO * tile * frames + 4 * block) // 8
        plan = text_plan(n_ha, n_wa, 2 * text // 8, width)
        received = []
        for _, _, rows, wide, _ in plan:
            received.append(pltpu.VMEM((rows, 8, wide), F32))
        sem = pltpu.SemaphoreType.DMA
        vmem = pl.BlockSpec(memory_space=pltpu.VMEM)
        outs = (
            jax.ShapeDtypeStruct(queries.shape, BF16),
            jax.ShapeDtypeStruct(queries.shape, BF16),
            jax.ShapeDtypeStruct(queries.shape, BF16),
            jax.ShapeDtypeStruct(text_keys.shape, BF16),
            jax.ShapeDtypeStruct(text_keys.shape, BF16),
        )
        results = pl.pallas_call(
            functools.partial(kernel, n_ha, n_wa, plan),
            out_shape=outs,
            in_specs=[pl.BlockSpec(memory_space=pltpu.SMEM)] + [vmem] * 8,
            out_specs=[vmem] * 5,
            scratch_shapes=[
                pltpu.VMEM((GROUPS, 2, 2, bands, block, part), BF16),
                pltpu.VMEM((GROUPS, 2, 2, bands, block, part), BF16),
                pltpu.VMEM((GROUPS, 2, 2, frames, HALO, tile, part), BF16),
                pltpu.VMEM((GROUPS, 2, 2, 2, block, part), BF16),
                pltpu.VMEM((GROUPS, 2, halo_blocks, 8, part), F32),
                pltpu.VMEM((GROUPS, 2, 2, 4, 8, part), F32),
                pltpu.VMEM((GROUPS, 2, 2, 2, 8, part), F32),
                pltpu.VMEM((GROUPS, 2, 2, bands, block, part), F32),
                pltpu.VMEM((2, cells, width), F32),
                pltpu.VMEM((cells, width), F32),
                pltpu.VMEM((8 * halo_blocks, cells), F32),
                pltpu.VMEM((heads, cells), F32),
                pltpu.VMEM((heads, cells), F32),
                pltpu.VMEM((2 * text // 8, 8, width), F32),
                pltpu.VMEM((2 * text // 8, 8, width), BF16),
                *received,
                sem((GROUPS, 2)), sem((GROUPS, 2)),
                sem((GROUPS, 2, 2)), sem((GROUPS, 2, 2)),
                sem((GROUPS, 2, 2)), sem((GROUPS, 2, 2)),
                sem((GROUPS, 2)), sem((GROUPS, 2)),
                sem((GROUPS, 2, 2)), sem((GROUPS, 2, 2)),
                sem((GROUPS, 2)), sem((GROUPS, 2)),
                sem((GROUPS, 2)), sem((GROUPS, 2)),
                sem((len(plan),)), sem((len(plan),)),
                sem((len(plan),)), sem((len(plan),)),
            ],
            compiler_params=pltpu.CompilerParams(
                collective_id=0, has_side_effects=True, vmem_limit_bytes=56 * 1024 * 1024
            ),
        )(
            window_table, queries, keys, values, out_grad,
            log_norm.transpose(1, 2, 3, 0).reshape(cells, heads), delta_rows.transpose(1, 2, 3, 0).reshape(cells, heads),
            text_keys, text_values,
        )

        return pl.pallas_call(
            hand_on,
            out_shape=outs,
            in_specs=[vmem] * 5,
            out_specs=[vmem] * 5,
        )(*results)

    tile_spec = P("group", "ha", "wa", None)
    stat_spec = P(None, "group", "ha", "wa")
    text_spec = P("group", None)
    return jax.shard_map(
        local,
        mesh=mesh,
        in_specs=(tile_spec,) * 4 + (stat_spec,) * 2 + (text_spec,) * 2 + (P(),),
        out_specs=(tile_spec,) * 3 + (text_spec,) * 2,
        check_vma=False,
    )
```

profile of v0, /device:TPU:0, one launch (start us, length us, event | category | flops | bytes accessed | tf_op | source)
XLA Modules:
  0.0 45.0 jit_solution(11831017784844602277)
XLA Ops:
  0.6 42.0 %shard_map.128 = (bf16[2,8,8,1536]{3,2,1,0:T(8,128)(2,1)}, bf16[2,8,8,1536]{3,2,1,0:T(8,128)(2,1)}, bf16[2,8,8,1536]{3,2,1,0:T(8,128)(2,1)}, bf16[32,1536]{1,0:T(8,128)(2,1)}, bf16[32,1536]{1,0:T(8,128)(2,1)}) custom-call(s32[4,4,9]{2,1,0:T(4,128)} %table.1, bf16[2,8,8,1536]{3,2,1,0:T(8,128)(2,1)} %q_ref.1, bf16[2,8,8,1536]{3,2,1,0:T(8,128)(2,1)} %k_ref.1, ...), custom_call_target="tpu_custom_call" | custom-call | tf_op jit(solution)/shard_map/pallas_call | solution.py:424
  42.6 2.4 %shard_map.129 = (bf16[2,8,8,1536]{3,2,1,0:T(8,128)(2,1)}, bf16[2,8,8,1536]{3,2,1,0:T(8,128)(2,1)}, bf16[2,8,8,1536]{3,2,1,0:T(8,128)(2,1)}, bf16[32,1536]{1,0:T(8,128)(2,1)}, bf16[32,1536]{1,0:T(8,128)(2,1)}) custom-call(bf16[2,8,8,1536]{3,2,1,0:T(8,128)(2,1)} %get-tuple-element.10.refs_0_, bf16[2,8,8,1536]{3,2,1,0:T(8,128)(2,1)} %get-tuple-element.11.refs_1_, ...), custom_call_target="tpu_custom_call" | custom-call | tf_op jit(solution)/shard_map/pallas_call | solution.py:465
where the time goes:
time: 45.2 us; the launch traced here: 45 us
  Pallas kernels  44.4 us (98%)
  between operations  0.64 us (1%)
    pallas_call x1, Pallas kernels, local(): pl.pallas_call(functools.partial(kernel, n_ha, n_wa, plan), out_shape=out...  42 us
    pallas_call x1, Pallas kernels, local(): pl.pallas_call(hand_on, out_shape=outs, in_specs=[vmem] * 5, out_specs=[v...  2.39 us

commit v1 on v0

v1 whole, which is shorter than its diff:
```python
import functools
import math

import jax
import jax.numpy as jnp
from jax import lax
from jax.experimental import pallas as pl
from jax.experimental.pallas import tpu as pltpu
from jax.sharding import PartitionSpec as P

HDIM = 128
HALO = 2
GROUPS = 4
MESH = pl.DeviceIdType.MESH
F32 = jnp.float32
BF16 = jnp.bfloat16
I16 = jnp.int16
STEPS = 32766.0
LEAST = 1e-30
LOG2E = math.log2(math.e)


def text_plan(n_ha, n_wa, blocks, width):
    plan = []

    def halve(axis, count):
        nonlocal blocks, width
        far = 1
        while far < count:
            if blocks > 1:
                blocks //= 2
                plan.append((axis, far, blocks, width, "rows"))
            elif width % 256 == 0:
                width //= 2
                plan.append((axis, far, blocks, width, "cols"))
            else:
                plan.append((axis, far, blocks, width, "none"))
            far *= 2

    halve("ha", n_ha)
    if width % (n_wa * 128) == 0:
        plan.append(("wa", n_wa, blocks, width // n_wa, "direct"))
    else:
        halve("wa", n_wa)
    return plan


def contract(a, b, dims):
    return lax.dot_general(a, b, (dims, ((), ())), preferred_element_type=F32)


def encode(x):
    most = jnp.maximum(jnp.max(jnp.abs(x), axis=0, keepdims=True), LEAST)
    codes = jnp.round(x * (STEPS / most)).astype(jnp.int32).astype(I16)
    return codes, most * (1.0 / STEPS)


def decode(codes, steps):
    return codes.astype(jnp.int32).astype(F32) * steps


def kernel(n_ha, n_wa, plan, *refs):
    (table_h, q_h, k_h, v_h, g_h, norm_h, delta_h, tk_h, tv_h) = refs[:9]
    (dq_ref, dk_ref, dv_ref, dtk_ref, dtv_ref) = refs[9:14]
    (
        table, q_ref, k_ref, v_ref, g_ref, norm_ref, delta_ref, tk_ref, tv_ref,
        stage, hcol, hrow, hcor, part_col,
        out_col, out_row, out_cor, in_col, in_row, in_cor,
        st_col, st_row, st_cor, sr_col, sr_row, sr_cor,
        own, dq_acc, mask, norm, delta, tx, tb,
    ) = refs[14:47]
    trecv = refs[47:47 + len(plan)]
    (
        load_s, col_s, col_r, row_s, row_r, cor_s, cor_r,
        mid_s, mid_r, rr_s, rr_r, rq_s, rq_r, end_s, end_r,
        t_s, t_r, u_s, u_r,
    ) = refs[47 + len(plan):]

    frames, plane, width = q_ref.shape
    tile = math.isqrt(plane)
    cells = frames * plane
    text = tk_ref.shape[0]
    heads = width // HDIM
    part = width // GROUPS
    per = heads // GROUPS
    bands = tile // HALO
    band = frames * HALO * HALO
    strip = bands * band
    rim = frames * HALO * tile
    scale = 1.0 / math.sqrt(HDIM)
    ha, wa = lax.axis_index("ha"), lax.axis_index("wa")
    ha_of = [{"ha": lax.rem(ha + n_ha - 1, n_ha)}, {"ha": lax.rem(ha + 1, n_ha)}]
    wa_of = [{"wa": lax.rem(wa + n_wa - 1, n_wa)}, {"wa": lax.rem(wa + 1, n_wa)}]

    partners, bits = [], []
    for axis, far, _, _, how in plan:
        at = ha if axis == "ha" else wa
        if how == "direct":
            bits.append(None)
            partners.append([{axis: lax.rem(at + hop, far)} for hop in range(1, far)])
        else:
            bit = lax.rem(lax.div(at, far), 2)
            bits.append(bit)
            partners.append([{axis: at + far * (1 - 2 * bit)}])

    barrier = pltpu.get_barrier_semaphore()
    greeted = ha_of + wa_of + sum(partners, [])
    for other in greeted:
        pl.semaphore_signal(barrier, inc=1, device_id=other, device_id_type=MESH)

    loads = []
    for n, (src, dst) in enumerate((
        (k_h, k_ref), (v_h, v_ref), (q_h, q_ref), (g_h, g_ref), (tk_h, tk_ref), (tv_h, tv_ref),
        (norm_h, norm_ref), (delta_h, delta_ref), (table_h, table),
    )):
        c = pltpu.make_async_copy(src, dst, load_s.at[n])
        c.start()
        loads.append(c)

    def cols(g):
        return slice(g * part, (g + 1) * part)

    def lanes(h):
        return slice(h * HDIM, (h + 1) * HDIM)

    def remote(src, dst, s, r, device):
        c = pltpu.make_async_remote_copy(
            src_ref=src, dst_ref=dst, send_sem=s, recv_sem=r, device_id=device, device_id_type=MESH
        )
        c.start()
        return c

    def cell_of(j):
        side = lax.div(j, strip)
        at_band = lax.rem(lax.div(j, band), bands)
        frame = lax.rem(lax.div(j, HALO * HALO), frames)
        row = at_band * HALO + lax.rem(lax.div(j, HALO), HALO)
        col = lax.rem(j, HALO) + side * (tile - HALO)
        return frame * plane + row * tile + col

    border = 2 * strip
    lane = lax.broadcasted_iota(jnp.int32, (border, cells), 1)
    pick = (lane == cell_of(lax.broadcasted_iota(jnp.int32, (border, cells), 0))).astype(F32).astype(BF16)
    back_row = lax.broadcasted_iota(jnp.int32, (cells, 2 * border), 0)
    back_lane = lax.broadcasted_iota(jnp.int32, (cells, 2 * border), 1)
    put_back = (back_row == cell_of(lax.rem(back_lane, border))).astype(F32).astype(BF16)

    def whole(ref, where):
        return ref[:, :, where].reshape(cells, where.stop - where.start)

    col_copy, row_copy, cor_copy, mid_copy, rr_copy, rq_copy, end_copy = {}, {}, {}, {}, {}, {}, {}

    def send_rows(g):
        for v in range(2):
            lo = v * (tile - HALO) * tile
            for kv, ref in enumerate((k_ref, v_ref)):
                row_copy[g, v, kv] = remote(
                    ref.at[:, lo:lo + HALO * tile, cols(g)], hrow.at[g, kv, 1 - v],
                    row_s.at[g, v, kv], row_r.at[g, 1 - v, kv], ha_of[v],
                )

    def pick_cols(g):
        for kv, ref in enumerate((k_ref, v_ref)):
            found = contract(pick, whole(ref, cols(g)), ((1,), (0,))).astype(BF16)
            for d in range(2):
                stage[g, kv, d] = found[d * strip:(d + 1) * strip]

    def send_cols(g):
        for d in range(2):
            col_copy[g, d] = remote(
                stage.at[g, :, d], hcol.at[g, :, 1 - d], col_s.at[g, d], col_r.at[g, 1 - d], wa_of[d]
            )

    loads[0].wait()
    loads[1].wait()
    pick_cols(0)
    pl.semaphore_wait(barrier, len(greeted))
    send_cols(0)
    send_rows(0)
    for g in range(1, GROUPS):
        pick_cols(g)
        send_cols(g)
        send_rows(g)

    for c in loads[2:]:
        c.wait()
    square = (cells, cells)
    same = (lax.broadcasted_iota(jnp.int32, square, 0) == lax.broadcasted_iota(jnp.int32, square, 1)).astype(F32)
    for src, dst, times in ((norm_ref, norm, LOG2E), (delta_ref, delta, 1.0)):
        dst[...] = times * lax.dot_general(
            src[...], same, (((0,), (0,)), ((), ())), precision=lax.Precision.HIGHEST, preferred_element_type=F32
        )

    def live(block):
        return table[ha, wa, block].astype(F32)

    at = 0
    for block, rows in ((1, rim), (7, rim), (0, band), (2, band), (6, band), (8, band), (3, strip), (5, strip)):
        mask[at:at + rows, :] = jnp.full((rows, cells), live(block), F32)
        at += rows
    own_live = live(4)

    def attend(todo, masking, sink):
        ahead = []

        def finish(h, keys, s, dp, qh, gh):
            p = masking(jnp.exp2(s * (scale * LOG2E) - norm[h:h + 1, :]))
            ds = (p * (dp - delta[h:h + 1, :])).astype(BF16)
            dv = contract(p.astype(BF16), gh, ((1,), (0,)))
            dk = contract(ds, qh, ((1,), (0,)))
            dq = contract(ds, keys, ((0,), (0,)))
            sink(h, dq, dk, dv)

        for h, keys, values in todo:
            qh, gh = whole(q_ref, lanes(h)), whole(g_ref, lanes(h))
            s = contract(keys, qh, ((1,), (1,)))
            dp = contract(values, gh, ((1,), (1,)))
            ahead.append((h, keys, s, dp, qh, gh))
            if len(ahead) > 1:
                finish(*ahead.pop(0))
        for left in ahead:
            finish(*left)

    def local(g):
        todo = []
        for h in range(g * per, (g + 1) * per):
            keys, values = (
                jnp.concatenate([whole(ref, lanes(h)), more[:, lanes(h)]], 0)
                for ref, more in ((k_ref, tk_ref), (v_ref, tv_ref))
            )
            todo.append((h, keys, values))

        def masking(p):
            return jnp.concatenate([p[:cells] * own_live, p[cells:]], 0)

        def sink(h, dq, dk, dv):
            here = lanes(h)
            dq_acc[:, here] = dq
            own[0, :, here] = dk[:cells]
            own[1, :, here] = dv[:cells]
            tx[: text // 8, :, here] = (dk[cells:] * scale).reshape(text // 8, 8, HDIM)
            tx[text // 8:, :, here] = dv[cells:].reshape(text // 8, 8, HDIM)

        attend(todo, masking, sink)

    def halo(g, rows_of, weights, sink):
        todo = []
        for n in range(per):
            keys, values = (rows_of(kv, lanes(n)) for kv in range(2))
            todo.append((g * per + n, keys, values))

        def take(h, dq, dk, dv):
            dq_acc[:, lanes(h)] += dq
            sink(lanes(h - g * per), (dk, dv))

        attend(todo, lambda p: p * weights, take)

    def forward(g):
        for d in range(2):
            col_copy[g, d].wait()
        for d in range(2):
            for v in range(2):
                lo = v * (strip - band)
                to = ((1 - v) * 2 + d) * band
                cor_copy[g, d, v] = remote(
                    hcol.at[g, :, d, lo:lo + band], hcor.at[g, :, to:to + band],
                    cor_s.at[g, d, v], cor_r.at[g, d, 1 - v], ha_of[v],
                )

    def columns(g):
        def sink(here, grads):
            for kv in range(2):
                for d in range(2):
                    lo = d * strip
                    codes, steps = encode(grads[kv][lo + band:lo + strip - band])
                    out_col[g, d, kv, band:strip - band, here] = codes
                    st_col[g, d, 1, kv:kv + 1, here] = steps
                    for v in range(2):
                        at = lo + v * (strip - band)
                        part_col[g, d, v, kv, :, here] = grads[kv][at:at + band]

        halo(
            g, lambda kv, here: hcol[g, kv, :, :, here].reshape(border, HDIM), mask[2 * rim + 4 * band:], sink
        )
        for d in range(2):
            mid_copy[g, d] = (
                remote(
                    out_col.at[g, d, :, band:strip - band], in_col.at[g, 1 - d, :, band:strip - band],
                    mid_s.at[g, d, 0], mid_r.at[g, 1 - d, 0], wa_of[d],
                ),
                remote(
                    st_col.at[g, d, 1], sr_col.at[g, 1 - d, 1], mid_s.at[g, d, 1], mid_r.at[g, 1 - d, 1], wa_of[d]
                ),
            )

    def strips(g):
        for v in range(2):
            for kv in range(2):
                row_copy[g, v, kv].wait()

        def sink(here, grads):
            for kv in range(2):
                for v in range(2):
                    codes, steps = encode(grads[kv][v * rim:(v + 1) * rim])
                    out_row[g, v, kv, :, here] = codes
                    st_row[g, v, kv:kv + 1, here] = steps

        halo(
            g, lambda kv, here: hrow[g, kv, :, :, :, here].reshape(2 * rim, HDIM), mask[:2 * rim], sink
        )
        for v in range(2):
            rr_copy[g, v] = (
                remote(out_row.at[g, v], in_row.at[g, 1 - v], rr_s.at[g, v, 0], rr_r.at[g, 1 - v, 0], ha_of[v]),
                remote(st_row.at[g, v], sr_row.at[g, 1 - v], rr_s.at[g, v, 1], rr_r.at[g, 1 - v, 1], ha_of[v]),
            )

    def corners(g):
        for v in range(2):
            for d in range(2):
                cor_copy[g, d, v].wait()

        def sink(here, grads):
            for kv in range(2):
                for v in range(2):
                    codes, steps = encode(grads[kv][2 * v * band:2 * (v + 1) * band])
                    out_cor[g, v, kv, :, here] = codes
                    st_cor[g, v, kv:kv + 1, here] = steps

        halo(g, lambda kv, here: hcor[g, kv, :, here], mask[2 * rim:2 * rim + 4 * band], sink)
        for v in range(2):
            rq_copy[g, v] = (
                remote(out_cor.at[g, v], in_cor.at[g, 1 - v], rq_s.at[g, v, 0], rq_r.at[g, 1 - v, 0], ha_of[v]),
                remote(st_cor.at[g, v], sr_cor.at[g, 1 - v], rq_s.at[g, v, 1], rq_r.at[g, 1 - v, 1], ha_of[v]),
            )

    def fold_corners(g):
        for v in range(2):
            for c in rq_copy[g, v]:
                c.wait()
        for v in range(2):
            for kv in range(2):
                came = decode(in_cor[g, v, kv], sr_cor[g, v, kv:kv + 1])
                for d in range(2):
                    total = part_col[g, d, v, kv] + came[d * band:(d + 1) * band]
                    codes, steps = encode(total)
                    at = v * (strip - band)
                    out_col[g, d, kv, at:at + band, :] = codes
                    st_col[g, d, 2 * v, kv:kv + 1, :] = steps
        for v in range(2):
            for d in range(2):
                at = v * (strip - band)
                end_copy[g, d, v] = (
                    remote(
                        out_col.at[g, d, :, at:at + band], in_col.at[g, 1 - d, :, at:at + band],
                        end_s.at[g, d, v, 0], end_r.at[g, 1 - d, v, 0], wa_of[d],
                    ),
                    remote(
                        st_col.at[g, d, 2 * v], sr_col.at[g, 1 - d, 2 * v],
                        end_s.at[g, d, v, 1], end_r.at[g, 1 - d, v, 1], wa_of[d],
                    ),
                )

    def fold_rows(g):
        for v in range(2):
            for c in rr_copy[g, v]:
                c.wait()
        for v in range(2):
            for kv in range(2):
                came = decode(in_row[g, v, kv], sr_row[g, v, kv:kv + 1])
                for f in range(frames):
                    lo = f * plane + v * (tile - HALO) * tile
                    own[kv, lo:lo + HALO * tile, cols(g)] += came[f * HALO * tile:(f + 1) * HALO * tile]

    def finish_queries(g):
        dq_ref[:, cols(g)] = (dq_acc[:, cols(g)] * scale).astype(BF16)

    def fold_cols(g):
        for d in range(2):
            for c in mid_copy[g, d] + end_copy[g, d, 0] + end_copy[g, d, 1]:
                c.wait()
        for kv, out in enumerate((dk_ref, dv_ref)):
            came = []
            for d in range(2):
                for piece, lo, hi in ((0, 0, band), (1, band, strip - band), (2, strip - band, strip)):
                    came.append(decode(in_col[g, d, kv, lo:hi], sr_col[g, d, piece, kv:kv + 1]))
            came = jnp.concatenate(came, 0)
            first = came.astype(BF16)
            second = (came - first.astype(F32)).astype(BF16)
            total = own[kv, :, cols(g)] + contract(put_back, jnp.concatenate([first, second], 0), ((1,), (0,)))
            if kv == 0:
                total = total * scale
            out[:, cols(g)] = total.astype(BF16)

    region = {"row": 0, "rows": 2 * text // 8, "col": 0, "cols": width}
    sums, regions = [], []

    def area(ref, row, rows, col, wide):
        where = pl.ds(pl.multiple_of(col, 128), wide) if not isinstance(col, int) else pl.ds(col, wide)
        return ref.at[pl.ds(row, rows), :, where]

    def mine(ref):
        return area(ref, region["row"], region["rows"], region["col"], region["cols"])

    def text_send(i):
        _, far, rows, wide, how = plan[i]
        regions.append(dict(region))
        row, col, bit = region["row"], region["col"], bits[i]
        if how == "direct":
            out = []
            for hop in range(1, far):
                to = lax.rem(wa + hop, far)
                out.append(remote(
                    area(tx, row, rows, col + to * wide, wide), trecv[i].at[hop - 1],
                    t_s.at[i, hop - 1], t_r.at[i, hop - 1], partners[i][hop - 1],
                ))
            region.update(col=col + wa * wide, cols=wide)
            sums.append(out)
            return
        send_row, send_col = row, col
        if how == "rows":
            send_row = row + (1 - bit) * rows
            region.update(row=row + bit * rows, rows=rows)
        elif how == "cols":
            send_col = col + (1 - bit) * wide
            region.update(col=col + bit * wide, cols=wide)
        sums.append([remote(
            area(tx, send_row, rows, send_col, wide), trecv[i].at[0], t_s.at[i, 0], t_r.at[i, 0], partners[i][0]
        )])

    def text_add(i):
        kept = mine(tx)
        for n, c in enumerate(sums[i]):
            c.wait()
        total = kept[...]
        for n in range(len(sums[i])):
            total = total + trecv[i][n]
        kept[...] = total

    gathers = []

    def text_spread(i):
        if i == len(plan) - 1:
            mine(tb)[...] = mine(tx)[...].astype(BF16)
        out = []
        if plan[i][4] != "none":
            for n, partner in enumerate(partners[i]):
                out.append(remote(mine(tb), mine(tb), u_s.at[i, n], u_r.at[i, n], partner))
        gathers.append(out)

    def text_join(i):
        for c in gathers.pop():
            c.wait()
        region.update(regions[i])

    steps = []
    for i in range(len(plan)):
        steps += [functools.partial(text_send, i), functools.partial(text_add, i)]
    for i in reversed(range(len(plan))):
        steps += [functools.partial(text_spread, i), functools.partial(text_join, i)]
    waiting = [steps[:1]] + [steps[n:n + 2] for n in range(1, len(steps) - 1, 2)] + [steps[-1:]]

    def text_step():
        if waiting:
            for step in waiting.pop(0):
                step()

    for g in range(GROUPS):
        local(g)
    text_step()
    strips(0)
    forward(0)
    columns(0)
    text_step()
    strips(1)
    forward(1)
    columns(1)
    corners(0)
    text_step()
    strips(2)
    forward(2)
    columns(2)
    fold_corners(0)
    corners(1)
    strips(3)
    forward(3)
    columns(3)
    text_step()
    fold_corners(1)
    corners(2)
    for g in range(GROUPS):
        fold_rows(g)
    fold_corners(2)
    corners(3)
    text_step()
    for g in range(GROUPS):
        finish_queries(g)
    fold_corners(3)
    while waiting:
        text_step()
    dtk_ref[...] = tb[: text // 8].astype(F32).reshape(text, width).astype(BF16)
    dtv_ref[...] = tb[text // 8:].astype(F32).reshape(text, width).astype(BF16)
    for g in range(GROUPS):
        fold_cols(g)


def hand_on(*refs):
    count = (len(refs) - 1) // 2
    copies = []
    for n in range(count):
        c = pltpu.make_async_copy(refs[n], refs[count + n], refs[-1].at[n])
        c.start()
        copies.append(c)
    for c in copies:
        c.wait()


def solution(mesh):
    n_ha, n_wa = mesh.shape["ha"], mesh.shape["wa"]

    def local(queries, keys, values, out_grad, log_norm, delta_rows, text_keys, text_values, window_table):
        frames, tile, _, width = queries.shape
        heads = width // HDIM
        text = text_keys.shape[0]
        plane = tile * tile
        cells = frames * plane
        part = width // GROUPS
        bands = tile // HALO
        band = frames * HALO * HALO
        strip = bands * band
        rim = frames * HALO * tile
        plan = text_plan(n_ha, n_wa, 2 * text // 8, width)
        most = max([far - 1 if how == "direct" else 1 for _, far, _, _, how in plan] + [1])
        received = []
        for _, far, rows, wide, how in plan:
            received.append(pltpu.VMEM((far - 1 if how == "direct" else 1, rows, 8, wide), F32))
        sem = pltpu.SemaphoreType.DMA
        anywhere = pl.BlockSpec(memory_space=pltpu.HBM)
        vmem = pl.BlockSpec(memory_space=pltpu.VMEM)
        rows = frames * plane
        results = pl.pallas_call(
            functools.partial(kernel, n_ha, n_wa, plan),
            out_shape=[pltpu.VMEM((rows, width), BF16)] * 3 + [pltpu.VMEM((text, width), BF16)] * 2,
            in_specs=[anywhere] * 9,
            out_specs=[vmem] * 5,
            scratch_shapes=[
                pltpu.SMEM(window_table.shape, jnp.int32),
                *[pltpu.VMEM((frames, plane, width), BF16)] * 4,
                *[pltpu.VMEM((cells, heads), F32)] * 2,
                *[pltpu.VMEM((text, width), BF16)] * 2,
                pltpu.VMEM((GROUPS, 2, 2, strip, part), BF16),
                pltpu.VMEM((GROUPS, 2, 2, strip, part), BF16),
                pltpu.VMEM((GROUPS, 2, 2, frames, HALO * tile, part), BF16),
                pltpu.VMEM((GROUPS, 2, 4 * band, part), BF16),
                pltpu.VMEM((GROUPS, 2, 2, 2, band, part), F32),
                pltpu.VMEM((GROUPS, 2, 2, strip, part), I16),
                pltpu.VMEM((GROUPS, 2, 2, rim, part), I16),
                pltpu.VMEM((GROUPS, 2, 2, 2 * band, part), I16),
                pltpu.VMEM((GROUPS, 2, 2, strip, part), I16),
                pltpu.VMEM((GROUPS, 2, 2, rim, part), I16),
                pltpu.VMEM((GROUPS, 2, 2, 2 * band, part), I16),
                pltpu.VMEM((GROUPS, 2, 3, 2, part), F32),
                pltpu.VMEM((GROUPS, 2, 2, part), F32),
                pltpu.VMEM((GROUPS, 2, 2, part), F32),
                pltpu.VMEM((GROUPS, 2, 3, 2, part), F32),
                pltpu.VMEM((GROUPS, 2, 2, part), F32),
                pltpu.VMEM((GROUPS, 2, 2, part), F32),
                pltpu.VMEM((2, cells, width), F32),
                pltpu.VMEM((cells, width), F32),
                pltpu.VMEM((2 * rim + 4 * band + 2 * strip, cells), F32),
                pltpu.VMEM((heads, cells), F32),
                pltpu.VMEM((heads, cells), F32),
                pltpu.VMEM((2 * text // 8, 8, width), F32),
                pltpu.VMEM((2 * text // 8, 8, width), BF16),
                *received,
                sem((9,)),
                sem((GROUPS, 2)), sem((GROUPS, 2)),
                sem((GROUPS, 2, 2)), sem((GROUPS, 2, 2)),
                sem((GROUPS, 2, 2)), sem((GROUPS, 2, 2)),
                sem((GROUPS, 2, 2)), sem((GROUPS, 2, 2)),
                sem((GROUPS, 2, 2)), sem((GROUPS, 2, 2)),
                sem((GROUPS, 2, 2)), sem((GROUPS, 2, 2)),
                sem((GROUPS, 2, 2, 2)), sem((GROUPS, 2, 2, 2)),
                sem((len(plan), most)), sem((len(plan), most)),
                sem((len(plan), most)), sem((len(plan), most)),
            ],
            compiler_params=pltpu.CompilerParams(
                collective_id=0, has_side_effects=True, vmem_limit_bytes=32 * 1024 * 1024
            ),
        )(*(
            pltpu.with_memory_space_constraint(x, pltpu.HBM) for x in (
                window_table,
                *(x.reshape(frames, plane, width) for x in (queries, keys, values, out_grad)),
                *(x.transpose(1, 2, 3, 0).reshape(cells, heads) for x in (log_norm, delta_rows)),
                text_keys, text_values,
            )
        ))

        dq, dk, dv, dtk, dtv = pl.pallas_call(
            hand_on,
            out_shape=[jax.ShapeDtypeStruct((rows, width), BF16)] * 3 + [jax.ShapeDtypeStruct((text, width), BF16)] * 2,
            in_specs=[vmem] * 5,
            out_specs=[anywhere] * 5,
            scratch_shapes=[sem((5,))],
            compiler_params=pltpu.CompilerParams(vmem_limit_bytes=4 * 1024 * 1024),
        )(*(pltpu.with_memory_space_constraint(x, pltpu.VMEM) for x in results))
        return *(x.reshape(queries.shape) for x in (dq, dk, dv)), dtk, dtv

    tile_spec = P("group", "ha", "wa", None)
    stat_spec = P(None, "group", "ha", "wa")
    text_spec = P("group", None)
    return jax.shard_map(
        local,
        mesh=mesh,
        in_specs=(tile_spec,) * 4 + (stat_spec,) * 2 + (text_spec,) * 2 + (P(),),
        out_specs=(tile_spec,) * 3 + (text_spec,) * 2,
        check_vma=False,
    )
```

time: 45.2 us -> 36.3 us (0.80)
  Pallas kernels: 44.4 us -> 35.6 us
    pallas_call x2, Pallas kernels: 44.4 us -> 35.6 us  [the longest x1 34.4 us: local(): pl.pallas_call(functools.partial(kernel, n_ha, n_wa, plan), out_shape=[pl...]
where the time goes in v1:
time: 36.3 us; the launch traced here: 36.2 us
  Pallas kernels  35.6 us (98%)
  between operations  0.64 us (2%)
    pallas_call x1, Pallas kernels, local(): pl.pallas_call(functools.partial(kernel, n_ha, n_wa, plan), out_shape=[pl...  34.4 us
    pallas_call x1, Pallas kernels, local(): pl.pallas_call(hand_on, out_shape=[jax.ShapeDtypeStruct((rows, width), BF...  1.11 us

profile of v1, /device:TPU:0, one launch (start us, length us, event | category | flops | bytes accessed | tf_op | source)
XLA Modules:
  0.0 36.2 jit_solution(8909480269350891955)
XLA Ops:
  0.6 34.4 %shard_map.128 = (bf16[128,1536]{1,0:T(8,128)(2,1)S(1)}, bf16[128,1536]{1,0:T(8,128)(2,1)S(1)}, bf16[128,1536]{1,0:T(8,128)(2,1)S(1)}, bf16[32,1536]{1,0:T(8,128)(2,1)S(1)}, bf16[32,1536]{1,0:T(8,128)(2,1)S(1)}) custom-call(s32[4,4,9]{2,1,0:T(4,128)} %refs_0_.1, bf16[2,64,1536]{2,1,0:T(8,128)(2,1)} %bitcast.13, bf16[2,64,1536]{2,1,0:T(8,128)(2,1)} %bitcast.14, ...), custom_call_target="tpu_custom_call" | custom-call | tf_op jit(solution)/shard_map/pallas_call | solution.py:540
  35.1 1.1 %shard_map.129 = (bf16[128,1536]{1,0:T(8,128)(2,1)}, bf16[128,1536]{1,0:T(8,128)(2,1)}, bf16[128,1536]{1,0:T(8,128)(2,1)}, bf16[32,1536]{1,0:T(8,128)(2,1)}, bf16[32,1536]{1,0:T(8,128)(2,1)}) custom-call(bf16[128,1536]{1,0:T(8,128)(2,1)S(1)} %get-tuple-element.15.refs_0_, bf16[128,1536]{1,0:T(8,128)(2,1)S(1)} %get-tuple-element.16.refs_1_, ...), custom_call_target="tpu_custom_call" | custom-call | tf_op jit(solution)/shard_map/pallas_call | solution.py:598

commit v2 on v1

--- a/solution.py
+++ b/solution.py
@@ -17,6 +17,7 @@
 I16 = jnp.int16
 STEPS = 32766.0
 LEAST = 1e-30
+AHEAD = 2
 LOG2E = math.log2(math.e)
 
 
@@ -45,6 +46,11 @@
     return plan
 
 
+def coded(stage_of):
+    axis, far, _, _, _ = stage_of
+    return axis != "ha" or far > 1
+
+
 def contract(a, b, dims):
     return lax.dot_general(a, b, (dims, ((), ())), preferred_element_type=F32)
 
@@ -69,12 +75,16 @@
         st_col, st_row, st_cor, sr_col, sr_row, sr_cor,
         own, dq_acc, mask, norm, delta, tx, tb,
     ) = refs[14:47]
-    trecv = refs[47:47 + len(plan)]
+    buffers, rest = [], refs[47:]
+    for stage_of in plan:
+        count = 4 if coded(stage_of) else 1
+        buffers.append(rest[:count])
+        rest = rest[count:]
     (
         load_s, col_s, col_r, row_s, row_r, cor_s, cor_r,
-        mid_s, mid_r, rr_s, rr_r, rq_s, rq_r, end_s, end_r,
+        rc_s, rc_r, rr_s, rr_r, rq_s, rq_r,
         t_s, t_r, u_s, u_r,
-    ) = refs[47 + len(plan):]
+    ) = rest
 
     frames, plane, width = q_ref.shape
     tile = math.isqrt(plane)
@@ -132,7 +142,8 @@
 
     def cell_of(j):
         side = lax.div(j, strip)
-        at_band = lax.rem(lax.div(j, band), bands)
+        order = lax.rem(lax.div(j, band), bands)
+        at_band = jnp.where(order == 0, 0, jnp.where(order == 1, bands - 1, order - 1))
         frame = lax.rem(lax.div(j, HALO * HALO), frames)
         row = at_band * HALO + lax.rem(lax.div(j, HALO), HALO)
         col = lax.rem(j, HALO) + side * (tile - HALO)
@@ -148,7 +159,7 @@
     def whole(ref, where):
         return ref[:, :, where].reshape(cells, where.stop - where.start)
 
-    col_copy, row_copy, cor_copy, mid_copy, rr_copy, rq_copy, end_copy = {}, {}, {}, {}, {}, {}, {}
+    col_copy, row_copy, cor_copy, rc_copy, rr_copy, rq_copy = {}, {}, {}, {}, {}, {}
 
     def send_rows(g):
         for v in range(2):
@@ -165,22 +176,26 @@
             for d in range(2):
                 stage[g, kv, d] = found[d * strip:(d + 1) * strip]
 
-    def send_cols(g):
+    def send_cols(g, half):
+        lo, hi = ((0, 2 * band), (2 * band, strip))[half]
         for d in range(2):
-            col_copy[g, d] = remote(
-                stage.at[g, :, d], hcol.at[g, :, 1 - d], col_s.at[g, d], col_r.at[g, 1 - d], wa_of[d]
+            col_copy[g, d, half] = remote(
+                stage.at[g, :, d, lo:hi], hcol.at[g, :, 1 - d, lo:hi],
+                col_s.at[g, d, half], col_r.at[g, 1 - d, half], wa_of[d],
             )
 
     loads[0].wait()
     loads[1].wait()
     pick_cols(0)
     pl.semaphore_wait(barrier, len(greeted))
-    send_cols(0)
+    send_cols(0, 0)
     send_rows(0)
     for g in range(1, GROUPS):
         pick_cols(g)
-        send_cols(g)
+        send_cols(g, 0)
         send_rows(g)
+    for g in range(GROUPS):
+        send_cols(g, 1)
 
     for c in loads[2:]:
         c.wait()
@@ -201,29 +216,32 @@
     own_live = live(4)
 
     def attend(todo, masking, sink):
-        ahead = []
-
-        def finish(h, keys, s, dp, qh, gh):
+        def scores(h, keys, values):
+            qh, gh = whole(q_ref, lanes(h)), whole(g_ref, lanes(h))
+            return h, keys, qh, gh, contract(keys, qh, ((1,), (1,))), contract(values, gh, ((1,), (1,)))
+
+        def grads(h, keys, qh, gh, s, dp):
             p = masking(jnp.exp2(s * (scale * LOG2E) - norm[h:h + 1, :]))
             ds = (p * (dp - delta[h:h + 1, :])).astype(BF16)
             dv = contract(p.astype(BF16), gh, ((1,), (0,)))
             dk = contract(ds, qh, ((1,), (0,)))
-            dq = contract(ds, keys, ((0,), (0,)))
-            sink(h, dq, dk, dv)
-
-        for h, keys, values in todo:
-            qh, gh = whole(q_ref, lanes(h)), whole(g_ref, lanes(h))
-            s = contract(keys, qh, ((1,), (1,)))
-            dp = contract(values, gh, ((1,), (1,)))
-            ahead.append((h, keys, s, dp, qh, gh))
-            if len(ahead) > 1:
-                finish(*ahead.pop(0))
-        for left in ahead:
-            finish(*left)
-
-    def local(g):
+            return h, keys, ds, dk, dv
+
+        def close(h, keys, ds, dk, dv):
+            sink(h, contract(ds, keys, ((0,), (0,))), dk, dv)
+
+        first, second = [], []
+        for n in range(len(todo) + AHEAD + 1):
+            if n < len(todo):
+                first.append(scores(*todo[n]))
+            if AHEAD <= n < len(todo) + AHEAD:
+                second.append(grads(*first.pop(0)))
+            if n > AHEAD:
+                close(*second.pop(0))
+
+    def local():
         todo = []
-        for h in range(g * per, (g + 1) * per):
+        for h in range(heads):
             keys, values = (
                 jnp.concatenate([whole(ref, lanes(h)), more[:, lanes(h)]], 0)
                 for ref, more in ((k_ref, tk_ref), (v_ref, tv_ref))
@@ -243,62 +261,84 @@
 
         attend(todo, masking, sink)
 
-    def halo(g, rows_of, weights, sink):
+    def halo(groups, rows_of, weights, sink):
         todo = []
-        for n in range(per):
-            keys, values = (rows_of(kv, lanes(n)) for kv in range(2))
-            todo.append((g * per + n, keys, values))
+        for g in groups:
+            for n in range(per):
+                keys, values = (rows_of(g, kv, lanes(n)) for kv in range(2))
+                todo.append((g * per + n, keys, values))
 
         def take(h, dq, dk, dv):
             dq_acc[:, lanes(h)] += dq
-            sink(lanes(h - g * per), (dk, dv))
+            sink(h // per, lanes(h % per), (dk, dv))
 
         attend(todo, lambda p: p * weights, take)
 
     def forward(g):
         for d in range(2):
-            col_copy[g, d].wait()
+            col_copy[g, d, 0].wait()
         for d in range(2):
             for v in range(2):
-                lo = v * (strip - band)
                 to = ((1 - v) * 2 + d) * band
                 cor_copy[g, d, v] = remote(
-                    hcol.at[g, :, d, lo:lo + band], hcor.at[g, :, to:to + band],
+                    hcol.at[g, :, d, v * band:(v + 1) * band], hcor.at[g, :, to:to + band],
                     cor_s.at[g, d, v], cor_r.at[g, d, 1 - v], ha_of[v],
                 )
 
-    def columns(g):
-        def sink(here, grads):
+    def columns(*groups):
+        for g in groups:
+            for d in range(2):
+                col_copy[g, d, 1].wait()
+
+        def sink(g, here, grads):
             for kv in range(2):
                 for d in range(2):
                     lo = d * strip
-                    codes, steps = encode(grads[kv][lo + band:lo + strip - band])
-                    out_col[g, d, kv, band:strip - band, here] = codes
+                    codes, steps = encode(grads[kv][lo + 2 * band:lo + strip])
+                    out_col[g, d, kv, 2 * band:, here] = codes
                     st_col[g, d, 1, kv:kv + 1, here] = steps
-                    for v in range(2):
-                        at = lo + v * (strip - band)
-                        part_col[g, d, v, kv, :, here] = grads[kv][at:at + band]
+                    part_col[g, d, kv, :, here] = grads[kv][lo:lo + 2 * band]
 
         halo(
-            g, lambda kv, here: hcol[g, kv, :, :, here].reshape(border, HDIM), mask[2 * rim + 4 * band:], sink
+            groups, lambda g, kv, here: hcol[g, kv, :, :, here].reshape(border, HDIM), mask[2 * rim + 4 * band:], sink
         )
+        for g in groups:
+            send_back(g, 1)
+
+    def send_back(g, half):
+        lo, hi = ((0, 2 * band), (2 * band, strip))[half]
         for d in range(2):
-            mid_copy[g, d] = (
+            rc_copy[g, d, half] = (
                 remote(
-                    out_col.at[g, d, :, band:strip - band], in_col.at[g, 1 - d, :, band:strip - band],
-                    mid_s.at[g, d, 0], mid_r.at[g, 1 - d, 0], wa_of[d],
+                    out_col.at[g, d, :, lo:hi], in_col.at[g, 1 - d, :, lo:hi],
+                    rc_s.at[g, d, half, 0], rc_r.at[g, 1 - d, half, 0], wa_of[d],
                 ),
                 remote(
-                    st_col.at[g, d, 1], sr_col.at[g, 1 - d, 1], mid_s.at[g, d, 1], mid_r.at[g, 1 - d, 1], wa_of[d]
+                    st_col.at[g, d, half], sr_col.at[g, 1 - d, half],
+                    rc_s.at[g, d, half, 1], rc_r.at[g, 1 - d, half, 1], wa_of[d],
                 ),
             )
 
-    def strips(g):
+    def fold_ends(g):
         for v in range(2):
-            for kv in range(2):
-                row_copy[g, v, kv].wait()
-
-        def sink(here, grads):
+            for c in rq_copy[g, v]:
+                c.wait()
+        for kv in range(2):
+            came = [decode(in_cor[g, v, kv], sr_cor[g, v, kv:kv + 1]) for v in range(2)]
+            for d in range(2):
+                ends = jnp.concatenate([came[v][d * band:(d + 1) * band] for v in range(2)], 0)
+                codes, steps = encode(part_col[g, d, kv] + ends)
+                out_col[g, d, kv, :2 * band, :] = codes
+                st_col[g, d, 0, kv:kv + 1, :] = steps
+        send_back(g, 0)
+
+    def strips(*groups):
+        for g in groups:
+            for v in range(2):
+                for kv in range(2):
+                    row_copy[g, v, kv].wait()
+
+        def sink(g, here, grads):
             for kv in range(2):
                 for v in range(2):
                     codes, steps = encode(grads[kv][v * rim:(v + 1) * rim])
@@ -306,58 +346,35 @@
                     st_row[g, v, kv:kv + 1, here] = steps
 
         halo(
-            g, lambda kv, here: hrow[g, kv, :, :, :, here].reshape(2 * rim, HDIM), mask[:2 * rim], sink
+            groups, lambda g, kv, here: hrow[g, kv, :, :, :, here].reshape(2 * rim, HDIM), mask[:2 * rim], sink
         )
+
+    def send_strips(g):
         for v in range(2):
             rr_copy[g, v] = (
                 remote(out_row.at[g, v], in_row.at[g, 1 - v], rr_s.at[g, v, 0], rr_r.at[g, 1 - v, 0], ha_of[v]),
                 remote(st_row.at[g, v], sr_row.at[g, 1 - v], rr_s.at[g, v, 1], rr_r.at[g, 1 - v, 1], ha_of[v]),
             )
 
-    def corners(g):
-        for v in range(2):
-            for d in range(2):
-                cor_copy[g, d, v].wait()
-
-        def sink(here, grads):
+    def corners(*groups):
+        for g in groups:
+            for v in range(2):
+                for d in range(2):
+                    cor_copy[g, d, v].wait()
+
+        def sink(g, here, grads):
             for kv in range(2):
                 for v in range(2):
                     codes, steps = encode(grads[kv][2 * v * band:2 * (v + 1) * band])
                     out_cor[g, v, kv, :, here] = codes
                     st_cor[g, v, kv:kv + 1, here] = steps
 
-        halo(g, lambda kv, here: hcor[g, kv, :, here], mask[2 * rim:2 * rim + 4 * band], sink)
-        for v in range(2):
-            rq_copy[g, v] = (
-                remote(out_cor.at[g, v], in_cor.at[g, 1 - v], rq_s.at[g, v, 0], rq_r.at[g, 1 - v, 0], ha_of[v]),
-                remote(st_cor.at[g, v], sr_cor.at[g, 1 - v], rq_s.at[g, v, 1], rq_r.at[g, 1 - v, 1], ha_of[v]),
-            )
-
-    def fold_corners(g):
-        for v in range(2):
-            for c in rq_copy[g, v]:
-                c.wait()
-        for v in range(2):
-            for kv in range(2):
-                came = decode(in_cor[g, v, kv], sr_cor[g, v, kv:kv + 1])
-                for d in range(2):
-                    total = part_col[g, d, v, kv] + came[d * band:(d + 1) * band]
-                    codes, steps = encode(total)
-                    at = v * (strip - band)
-                    out_col[g, d, kv, at:at + band, :] = codes
-                    st_col[g, d, 2 * v, kv:kv + 1, :] = steps
-        for v in range(2):
-            for d in range(2):
-                at = v * (strip - band)
-                end_copy[g, d, v] = (
-                    remote(
-                        out_col.at[g, d, :, at:at + band], in_col.at[g, 1 - d, :, at:at + band],
-                        end_s.at[g, d, v, 0], end_r.at[g, 1 - d, v, 0], wa_of[d],
-                    ),
-                    remote(
-                        st_col.at[g, d, 2 * v], sr_col.at[g, 1 - d, 2 * v],
-                        end_s.at[g, d, v, 1], end_r.at[g, 1 - d, v, 1], wa_of[d],
-                    ),
+        halo(groups, lambda g, kv, here: hcor[g, kv, :, here], mask[2 * rim:2 * rim + 4 * band], sink)
+        for g in groups:
+            for v in range(2):
+                rq_copy[g, v] = (
+                    remote(out_cor.at[g, v], in_cor.at[g, 1 - v], rq_s.at[g, v, 0], rq_r.at[g, 1 - v, 0], ha_of[v]),
+                    remote(st_cor.at[g, v], sr_cor.at[g, 1 - v], rq_s.at[g, v, 1], rq_r.at[g, 1 - v, 1], ha_of[v]),
                 )
 
     def fold_rows(g):
@@ -376,14 +393,13 @@
 
     def fold_cols(g):
         for d in range(2):
-            for c in mid_copy[g, d] + end_copy[g, d, 0] + end_copy[g, d, 1]:
+            for c in rc_copy[g, d, 0] + rc_copy[g, d, 1]:
                 c.wait()
         for kv, out in enumerate((dk_ref, dv_ref)):
-            came = []
-            for d in range(2):
-                for piece, lo, hi in ((0, 0, band), (1, band, strip - band), (2, strip - band, strip)):
-                    came.append(decode(in_col[g, d, kv, lo:hi], sr_col[g, d, piece, kv:kv + 1]))
-            came = jnp.concatenate(came, 0)
+            came = jnp.concatenate([
+                decode(in_col[g, d, kv, lo:hi], sr_col[g, d, half, kv:kv + 1])
+                for d in range(2) for half, (lo, hi) in enumerate(((0, 2 * band), (2 * band, strip)))
+            ], 0)
             first = came.astype(BF16)
             second = (came - first.astype(F32)).astype(BF16)
             total = own[kv, :, cols(g)] + contract(put_back, jnp.concatenate([first, second], 0), ((1,), (0,)))
@@ -406,34 +422,40 @@
         regions.append(dict(region))
         row, col, bit = region["row"], region["col"], bits[i]
         if how == "direct":
-            out = []
-            for hop in range(1, far):
-                to = lax.rem(wa + hop, far)
-                out.append(remote(
-                    area(tx, row, rows, col + to * wide, wide), trecv[i].at[hop - 1],
-                    t_s.at[i, hop - 1], t_r.at[i, hop - 1], partners[i][hop - 1],
-                ))
+            where = [(row, col + lax.rem(wa + hop, far) * wide) for hop in range(1, far)]
             region.update(col=col + wa * wide, cols=wide)
-            sums.append(out)
-            return
-        send_row, send_col = row, col
-        if how == "rows":
-            send_row = row + (1 - bit) * rows
+        elif how == "rows":
+            where = [(row + (1 - bit) * rows, col)]
             region.update(row=row + bit * rows, rows=rows)
         elif how == "cols":
-            send_col = col + (1 - bit) * wide
+            where = [(row, col + (1 - bit) * wide)]
             region.update(col=col + bit * wide, cols=wide)
-        sums.append([remote(
-            area(tx, send_row, rows, send_col, wide), trecv[i].at[0], t_s.at[i, 0], t_r.at[i, 0], partners[i][0]
-        )])
+        else:
+            where = [(row, col)]
+        out = []
+        for n, at in enumerate(where):
+            source = area(tx, at[0], rows, at[1], wide)
+            if coded(plan[i]):
+                codes, steps, codes_in, steps_in = buffers[i]
+                codes[n], steps[n] = encode(source[...].reshape(rows * 8, wide))
+                out.append(remote(codes.at[n], codes_in.at[n], t_s.at[i, n, 0], t_r.at[i, n, 0], partners[i][n]))
+                out.append(remote(steps.at[n], steps_in.at[n], t_s.at[i, n, 1], t_r.at[i, n, 1], partners[i][n]))
+            else:
+                out.append(remote(source, buffers[i][0].at[n], t_s.at[i, n, 0], t_r.at[i, n, 0], partners[i][n]))
+        sums.append(out)
 
     def text_add(i):
+        _, _, rows, wide, _ = plan[i]
+        for c in sums[i]:
+            c.wait()
         kept = mine(tx)
-        for n, c in enumerate(sums[i]):
-            c.wait()
         total = kept[...]
-        for n in range(len(sums[i])):
-            total = total + trecv[i][n]
+        for n in range(len(partners[i])):
+            if coded(plan[i]):
+                _, _, codes_in, steps_in = buffers[i]
+                total = total + decode(codes_in[n], steps_in[n]).reshape(rows, 8, wide)
+            else:
+                total = total + buffers[i][0][n]
         kept[...] = total
 
     gathers = []
@@ -464,42 +486,48 @@
             for step in waiting.pop(0):
                 step()
 
-    for g in range(GROUPS):
-        local(g)
+    local()
     text_step()
     strips(0)
     forward(0)
-    columns(0)
     text_step()
     strips(1)
     forward(1)
-    columns(1)
-    corners(0)
-    text_step()
     strips(2)
     forward(2)
-    columns(2)
-    fold_corners(0)
-    corners(1)
     strips(3)
     forward(3)
+    text_step()
+    corners(0)
+    send_strips(0)
+    columns(0)
+    corners(1)
+    send_strips(1)
+    columns(1)
+    text_step()
+    corners(2)
+    send_strips(2)
+    fold_ends(0)
+    columns(2)
+    corners(3)
+    send_strips(3)
+    fold_ends(1)
     columns(3)
+    fold_ends(2)
     text_step()
-    fold_corners(1)
-    corners(2)
+    fold_ends(3)
+    for g in range(GROUPS):
+        finish_queries(g)
     for g in range(GROUPS):
         fold_rows(g)
-    fold_corners(2)
-    corners(3)
     text_step()
-    for g in range(GROUPS):
-        finish_queries(g)
-    fold_corners(3)
+    fold_cols(0)
+    fold_cols(1)
     while waiting:
         text_step()
     dtk_ref[...] = tb[: text // 8].astype(F32).reshape(text, width).astype(BF16)
     dtv_ref[...] = tb[text // 8:].astype(F32).reshape(text, width).astype(BF16)
-    for g in range(GROUPS):
+    for g in range(2, GROUPS):
         fold_cols(g)
 
 
@@ -531,8 +559,13 @@
         plan = text_plan(n_ha, n_wa, 2 * text // 8, width)
         most = max([far - 1 if how == "direct" else 1 for _, far, _, _, how in plan] + [1])
         received = []
-        for _, far, rows, wide, how in plan:
-            received.append(pltpu.VMEM((far - 1 if how == "direct" else 1, rows, 8, wide), F32))
+        for stage_of in plan:
+            _, far, rows, wide, how = stage_of
+            n = far - 1 if how == "direct" else 1
+            if coded(stage_of):
+                received += [pltpu.VMEM((n, rows * 8, wide), I16), pltpu.VMEM((n, 1, wide), F32)] * 2
+            else:
+                received.append(pltpu.VMEM((n, rows, 8, wide), F32))
         sem = pltpu.SemaphoreType.DMA
         anywhere = pl.BlockSpec(memory_space=pltpu.HBM)
         vmem = pl.BlockSpec(memory_space=pltpu.VMEM)
@@ -551,17 +584,17 @@
                 pltpu.VMEM((GROUPS, 2, 2, strip, part), BF16),
                 pltpu.VMEM((GROUPS, 2, 2, frames, HALO * tile, part), BF16),
                 pltpu.VMEM((GROUPS, 2, 4 * band, part), BF16),
-                pltpu.VMEM((GROUPS, 2, 2, 2, band, part), F32),
+                pltpu.VMEM((GROUPS, 2, 2, 2 * band, part), F32),
                 pltpu.VMEM((GROUPS, 2, 2, strip, part), I16),
                 pltpu.VMEM((GROUPS, 2, 2, rim, part), I16),
                 pltpu.VMEM((GROUPS, 2, 2, 2 * band, part), I16),
                 pltpu.VMEM((GROUPS, 2, 2, strip, part), I16),
                 pltpu.VMEM((GROUPS, 2, 2, rim, part), I16),
                 pltpu.VMEM((GROUPS, 2, 2, 2 * band, part), I16),
-                pltpu.VMEM((GROUPS, 2, 3, 2, part), F32),
+                pltpu.VMEM((GROUPS, 2, 2, 2, part), F32),
                 pltpu.VMEM((GROUPS, 2, 2, part), F32),
                 pltpu.VMEM((GROUPS, 2, 2, part), F32),
-                pltpu.VMEM((GROUPS, 2, 3, 2, part), F32),
+                pltpu.VMEM((GROUPS, 2, 2, 2, part), F32),
                 pltpu.VMEM((GROUPS, 2, 2, part), F32),
                 pltpu.VMEM((GROUPS, 2, 2, part), F32),
                 pltpu.VMEM((2, cells, width), F32),
@@ -573,14 +606,13 @@
                 pltpu.VMEM((2 * text // 8, 8, width), BF16),
                 *received,
                 sem((9,)),
-                sem((GROUPS, 2)), sem((GROUPS, 2)),
-                sem((GROUPS, 2, 2)), sem((GROUPS, 2, 2)),
-                sem((GROUPS, 2, 2)), sem((GROUPS, 2, 2)),
                 sem((GROUPS, 2, 2)), sem((GROUPS, 2, 2)),
                 sem((GROUPS, 2, 2)), sem((GROUPS, 2, 2)),
                 sem((GROUPS, 2, 2)), sem((GROUPS, 2, 2)),
                 sem((GROUPS, 2, 2, 2)), sem((GROUPS, 2, 2, 2)),
-                sem((len(plan), most)), sem((len(plan), most)),
+                sem((GROUPS, 2, 2)), sem((GROUPS, 2, 2)),
+                sem((GROUPS, 2, 2)), sem((GROUPS, 2, 2)),
+                sem((len(plan), most, 2)), sem((len(plan), most, 2)),
                 sem((len(plan), most)), sem((len(plan), most)),
             ],
             compiler_params=pltpu.CompilerParams(

time: 36.3 us -> 32 us (0.88)
  Pallas kernels: 35.6 us -> 31.2 us
    pallas_call x1, Pallas kernels: 34.4 us -> 30.1 us  [local(): pl.pallas_call(functools.partial(kernel, n_ha, n_wa, plan), out_shape=[pl...]
where the time goes in v2:
time: 32 us; the launch traced here: 31.8 us
  Pallas kernels  31.2 us (98%)
  between operations  0.64 us (2%)
    pallas_call x1, Pallas kernels, local(): pl.pallas_call(functools.partial(kernel, n_ha, n_wa, plan), out_shape=[pl...  30.1 us
    pallas_call x1, Pallas kernels, local(): pl.pallas_call(hand_on, out_shape=[jax.ShapeDtypeStruct((rows, width), BF...  1.11 us

profile of v2, /device:TPU:0, one launch (start us, length us, event | category | flops | bytes accessed | tf_op | source)
XLA Modules:
  0.0 31.8 jit_solution(17463273776645895564)
XLA Ops:
  0.6 30.1 %shard_map.128 = (bf16[128,1536]{1,0:T(8,128)(2,1)S(1)}, bf16[128,1536]{1,0:T(8,128)(2,1)S(1)}, bf16[128,1536]{1,0:T(8,128)(2,1)S(1)}, bf16[32,1536]{1,0:T(8,128)(2,1)S(1)}, bf16[32,1536]{1,0:T(8,128)(2,1)S(1)}) custom-call(s32[4,4,9]{2,1,0:T(4,128)} %refs_0_.1, bf16[2,64,1536]{2,1,0:T(8,128)(2,1)} %bitcast.13, bf16[2,64,1536]{2,1,0:T(8,128)(2,1)} %bitcast.14, ...), custom_call_target="tpu_custom_call" | custom-call | tf_op jit(solution)/shard_map/pallas_call | solution.py:573
  30.7 1.1 %shard_map.129 = (bf16[128,1536]{1,0:T(8,128)(2,1)}, bf16[128,1536]{1,0:T(8,128)(2,1)}, bf16[128,1536]{1,0:T(8,128)(2,1)}, bf16[32,1536]{1,0:T(8,128)(2,1)}, bf16[32,1536]{1,0:T(8,128)(2,1)}) custom-call(bf16[128,1536]{1,0:T(8,128)(2,1)S(1)} %get-tuple-element.15.refs_0_, bf16[128,1536]{1,0:T(8,128)(2,1)S(1)} %get-tuple-element.16.refs_1_, ...), custom_call_target="tpu_custom_call" | custom-call | tf_op jit(solution)/shard_map/pallas_call | solution.py:630

commit v3 on v2

--- a/solution.py
+++ b/solution.py
@@ -55,14 +55,24 @@
     return lax.dot_general(a, b, (dims, ((), ())), preferred_element_type=F32)
 
 
+def slices(x):
+    return [x[:, n:n + HDIM] for n in range(0, x.shape[1], HDIM)]
+
+
 def encode(x):
-    most = jnp.maximum(jnp.max(jnp.abs(x), axis=0, keepdims=True), LEAST)
-    codes = jnp.round(x * (STEPS / most)).astype(jnp.int32).astype(I16)
+    most = jnp.max(jnp.abs(x), axis=0, keepdims=True)
+    most = jnp.maximum(functools.reduce(jnp.maximum, slices(most)), LEAST)
+    by = STEPS / most
+    codes = jnp.concatenate([jnp.round(piece * by).astype(jnp.int32).astype(I16) for piece in slices(x)], 1)
     return codes, most * (1.0 / STEPS)
 
 
+def by_head(codes, steps):
+    return codes.astype(jnp.int32).astype(F32) * steps
+
+
 def decode(codes, steps):
-    return codes.astype(jnp.int32).astype(F32) * steps
+    return jnp.concatenate([piece.astype(jnp.int32).astype(F32) * steps for piece in slices(codes)], 1)
 
 
 def kernel(n_ha, n_wa, plan, *refs):
@@ -117,6 +127,7 @@
     greeted = ha_of + wa_of + sum(partners, [])
     for other in greeted:
         pl.semaphore_signal(barrier, inc=1, device_id=other, device_id_type=MESH)
+    last = jnp.where(wa < n_wa - 1, 0, 1)
 
     loads = []
     for n, (src, dst) in enumerate((
@@ -133,10 +144,13 @@
     def lanes(h):
         return slice(h * HDIM, (h + 1) * HDIM)
 
-    def remote(src, dst, s, r, device):
-        c = pltpu.make_async_remote_copy(
+    def later(src, dst, s, r, device):
+        return pltpu.make_async_remote_copy(
             src_ref=src, dst_ref=dst, send_sem=s, recv_sem=r, device_id=device, device_id_type=MESH
         )
+
+    def remote(*what):
+        c = later(*what)
         c.start()
         return c
 
@@ -178,10 +192,12 @@
 
     def send_cols(g, half):
         lo, hi = ((0, 2 * band), (2 * band, strip))[half]
-        for d in range(2):
-            col_copy[g, d, half] = remote(
+        for n in range(2):
+            d = lax.rem(last + n, 2)
+            to = {"wa": lax.rem(wa + n_wa + 2 * d - 1, n_wa)}
+            col_copy[g, n, half] = remote(
                 stage.at[g, :, d, lo:hi], hcol.at[g, :, 1 - d, lo:hi],
-                col_s.at[g, d, half], col_r.at[g, 1 - d, half], wa_of[d],
+                col_s.at[g, d, half], col_r.at[g, 1 - d, half], to,
             )
 
     loads[0].wait()
@@ -293,29 +309,32 @@
         def sink(g, here, grads):
             for kv in range(2):
                 for d in range(2):
-                    lo = d * strip
-                    codes, steps = encode(grads[kv][lo + 2 * band:lo + strip])
-                    out_col[g, d, kv, 2 * band:, here] = codes
-                    st_col[g, d, 1, kv:kv + 1, here] = steps
-                    part_col[g, d, kv, :, here] = grads[kv][lo:lo + 2 * band]
+                    part_col[g, d, kv, :, here] = grads[kv][d * strip:(d + 1) * strip]
 
         halo(
             groups, lambda g, kv, here: hcol[g, kv, :, :, here].reshape(border, HDIM), mask[2 * rim + 4 * band:], sink
         )
         for g in groups:
+            for kv in range(2):
+                for d in range(2):
+                    codes, steps = encode(part_col[g, d, kv, 2 * band:])
+                    out_col[g, d, kv, 2 * band:, :] = codes
+                    st_col[g, d, 1, kv:kv + 1, :] = steps
             send_back(g, 1)
 
     def send_back(g, half):
         lo, hi = ((0, 2 * band), (2 * band, strip))[half]
-        for d in range(2):
-            rc_copy[g, d, half] = (
+        for n in range(2):
+            d = lax.rem(last + n, 2)
+            to = {"wa": lax.rem(wa + n_wa + 2 * d - 1, n_wa)}
+            rc_copy[g, n, half] = (
                 remote(
                     out_col.at[g, d, :, lo:hi], in_col.at[g, 1 - d, :, lo:hi],
-                    rc_s.at[g, d, half, 0], rc_r.at[g, 1 - d, half, 0], wa_of[d],
+                    rc_s.at[g, d, half, 0], rc_r.at[g, 1 - d, half, 0], to,
                 ),
                 remote(
                     st_col.at[g, d, half], sr_col.at[g, 1 - d, half],
-                    rc_s.at[g, d, half, 1], rc_r.at[g, 1 - d, half, 1], wa_of[d],
+                    rc_s.at[g, d, half, 1], rc_r.at[g, 1 - d, half, 1], to,
                 ),
             )
 
@@ -324,10 +343,10 @@
             for c in rq_copy[g, v]:
                 c.wait()
         for kv in range(2):
-            came = [decode(in_cor[g, v, kv], sr_cor[g, v, kv:kv + 1]) for v in range(2)]
+            came = [by_head(in_cor[g, v, kv], sr_cor[g, v, kv:kv + 1]) for v in range(2)]
             for d in range(2):
                 ends = jnp.concatenate([came[v][d * band:(d + 1) * band] for v in range(2)], 0)
-                codes, steps = encode(part_col[g, d, kv] + ends)
+                codes, steps = encode(part_col[g, d, kv, :2 * band] + ends)
                 out_col[g, d, kv, :2 * band, :] = codes
                 st_col[g, d, 0, kv:kv + 1, :] = steps
         send_back(g, 0)
@@ -383,7 +402,7 @@
                 c.wait()
         for v in range(2):
             for kv in range(2):
-                came = decode(in_row[g, v, kv], sr_row[g, v, kv:kv + 1])
+                came = by_head(in_row[g, v, kv], sr_row[g, v, kv:kv + 1])
                 for f in range(frames):
                     lo = f * plane + v * (tile - HALO) * tile
                     own[kv, lo:lo + HALO * tile, cols(g)] += came[f * HALO * tile:(f + 1) * HALO * tile]
@@ -518,8 +537,10 @@
     fold_ends(3)
     for g in range(GROUPS):
         finish_queries(g)
-    for g in range(GROUPS):
-        fold_rows(g)
+    fold_rows(0)
+    fold_rows(1)
+    fold_rows(2)
+    fold_rows(3)
     text_step()
     fold_cols(0)
     fold_cols(1)
@@ -527,8 +548,8 @@
         text_step()
     dtk_ref[...] = tb[: text // 8].astype(F32).reshape(text, width).astype(BF16)
     dtv_ref[...] = tb[text // 8:].astype(F32).reshape(text, width).astype(BF16)
-    for g in range(2, GROUPS):
-        fold_cols(g)
+    fold_cols(2)
+    fold_cols(3)
 
 
 def hand_on(*refs):
@@ -563,7 +584,7 @@
             _, far, rows, wide, how = stage_of
             n = far - 1 if how == "direct" else 1
             if coded(stage_of):
-                received += [pltpu.VMEM((n, rows * 8, wide), I16), pltpu.VMEM((n, 1, wide), F32)] * 2
+                received += [pltpu.VMEM((n, rows * 8, wide), I16), pltpu.VMEM((n, 1, HDIM), F32)] * 2
             else:
                 received.append(pltpu.VMEM((n, rows, 8, wide), F32))
         sem = pltpu.SemaphoreType.DMA
@@ -584,17 +605,17 @@
                 pltpu.VMEM((GROUPS, 2, 2, strip, part), BF16),
                 pltpu.VMEM((GROUPS, 2, 2, frames, HALO * tile, part), BF16),
                 pltpu.VMEM((GROUPS, 2, 4 * band, part), BF16),
-                pltpu.VMEM((GROUPS, 2, 2, 2 * band, part), F32),
+                pltpu.VMEM((GROUPS, 2, 2, strip, part), F32),
                 pltpu.VMEM((GROUPS, 2, 2, strip, part), I16),
                 pltpu.VMEM((GROUPS, 2, 2, rim, part), I16),
                 pltpu.VMEM((GROUPS, 2, 2, 2 * band, part), I16),
                 pltpu.VMEM((GROUPS, 2, 2, strip, part), I16),
                 pltpu.VMEM((GROUPS, 2, 2, rim, part), I16),
                 pltpu.VMEM((GROUPS, 2, 2, 2 * band, part), I16),
-                pltpu.VMEM((GROUPS, 2, 2, 2, part), F32),
+                pltpu.VMEM((GROUPS, 2, 2, 2, HDIM), F32),
                 pltpu.VMEM((GROUPS, 2, 2, part), F32),
                 pltpu.VMEM((GROUPS, 2, 2, part), F32),
-                pltpu.VMEM((GROUPS, 2, 2, 2, part), F32),
+                pltpu.VMEM((GROUPS, 2, 2, 2, HDIM), F32),
                 pltpu.VMEM((GROUPS, 2, 2, part), F32),
                 pltpu.VMEM((GROUPS, 2, 2, part), F32),
                 pltpu.VMEM((2, cells, width), F32),

time: 32 us -> 31.1 us (0.972)
  Pallas kernels: 31.2 us -> 30.3 us
    pallas_call x1, Pallas kernels: 30.1 us -> 29.2 us  [local(): pl.pallas_call(functools.partial(kernel, n_ha, n_wa, plan), out_shape=[pl...]
where the time goes in v3:
time: 31.1 us; the launch traced here: 31 us
  Pallas kernels  30.3 us (97%)
  between operations  0.64 us (2%)
    pallas_call x1, Pallas kernels, local(): pl.pallas_call(functools.partial(kernel, n_ha, n_wa, plan), out_shape=[pl...  29.2 us
    pallas_call x1, Pallas kernels, local(): pl.pallas_call(hand_on, out_shape=[jax.ShapeDtypeStruct((rows, width), BF...  1.11 us

profile of v3, /device:TPU:0, one launch (start us, length us, event | category | flops | bytes accessed | tf_op | source)
XLA Modules:
  0.0 31.0 jit_solution(1002016594040967194)
XLA Ops:
  0.6 29.2 %shard_map.128 = (bf16[128,1536]{1,0:T(8,128)(2,1)S(1)}, bf16[128,1536]{1,0:T(8,128)(2,1)S(1)}, bf16[128,1536]{1,0:T(8,128)(2,1)S(1)}, bf16[32,1536]{1,0:T(8,128)(2,1)S(1)}, bf16[32,1536]{1,0:T(8,128)(2,1)S(1)}) custom-call(s32[4,4,9]{2,1,0:T(4,128)} %refs_0_.1, bf16[2,64,1536]{2,1,0:T(8,128)(2,1)} %bitcast.13, bf16[2,64,1536]{2,1,0:T(8,128)(2,1)} %bitcast.14, ...), custom_call_target="tpu_custom_call" | custom-call | tf_op jit(solution)/shard_map/pallas_call | solution.py:594
  29.9 1.1 %shard_map.129 = (bf16[128,1536]{1,0:T(8,128)(2,1)}, bf16[128,1536]{1,0:T(8,128)(2,1)}, bf16[128,1536]{1,0:T(8,128)(2,1)}, bf16[32,1536]{1,0:T(8,128)(2,1)}, bf16[32,1536]{1,0:T(8,128)(2,1)}) custom-call(bf16[128,1536]{1,0:T(8,128)(2,1)S(1)} %get-tuple-element.15.refs_0_, bf16[128,1536]{1,0:T(8,128)(2,1)S(1)} %get-tuple-element.16.refs_1_, ...), custom_call_target="tpu_custom_call" | custom-call | tf_op jit(solution)/shard_map/pallas_call | solution.py:651
